TPU v7x, 32 devices: a whole 2x2x4 slice. The times are simulated.
32 devices in a mesh: depth: 4 (over z), imgx: 4 (over y, core), imgy: 2 (over x).
Axes of the slice: x: 2, y: 2, z: 4, core: 2. Of those that a mesh axis runs over, the one named last changes fastest.
Arguments:
- emissivity: bfloat16 [32, 512, 256], P('depth', 'imgx', 'imgy'), may hold values from 0.099609375 to 10
- bin_index: int32 [32, 512, 256], P('depth', 'imgx', 'imgy'), may hold values from 0 to 127
- color_table: bfloat16 [4, 128], replicated, may hold values from 0.049804688 to 1
- brick_order: int32 [4], replicated, may hold values from 0 to 3, each once
Outputs:
- image: float32 [4, 512, 256], P(None, 'imgx', 'imgy')
Inputs may be any that keep to these rules, and one draw needn't show every extreme that they name: brick_order names every brick index once.
All inputs are finite; a program needn't handle non-finite values.
Results may differ from a plain program's by a relative error of at most 0.0003.
Values sent between devices are 32-bit elements; how exact they have to be, the bound alone decides.
No kernel may reach another device: no remote copies, remote signals or barrier semaphores. Data moves between devices by JAX's collectives and lax.ppermute only.
A program may use at most 64 MiB of HBM per device.

v0:
```python
import jax
import jax.numpy as jnp
from jax import lax
from jax.sharding import PartitionSpec as P


def on_device(emissivity, bin_index, color_table, brick_order):
    depth_cells, cols_x, cols_y = emissivity.shape
    pixels = cols_x * cols_y
    devices = lax.axis_size("depth")
    ray_step = 2.0 / (depth_cells * devices)
    levels = jnp.arange(color_table.shape[1], dtype=jnp.int32)

    def lookup(layer_bins):
        onehot = (layer_bins.reshape(1, pixels) == levels[:, None]).astype(jnp.bfloat16)
        return jnp.dot(color_table, onehot, preferred_element_type=jnp.float32)

    looked = lax.map(lookup, bin_index)
    bright = emissivity.reshape(depth_cells, pixels).astype(jnp.float32)
    glow_rgb = bright[:, None, :] * looked[:, 0:3, :]
    absorb_rate = bright * looked[:, 3, :]
    depth_in = jnp.cumsum(absorb_rate, axis=0) - absorb_rate
    light_in = jnp.exp(-ray_step * depth_in)
    color_sum = jnp.sum(ray_step * glow_rgb * light_in[:, None, :], axis=0)
    passed = jnp.exp(-ray_step * jnp.sum(absorb_rate, axis=0))
    piece_len = pixels // devices
    stacked = jnp.concatenate([color_sum, passed[None]], 0)[None]
    received = lax.all_to_all(stacked, "depth", split_axis=2, concat_axis=0, tiled=True)
    ordered = jnp.take(received, brick_order, axis=0)
    passed_all = ordered[:, 3, :]
    ahead_light = jnp.cumprod(
        jnp.concatenate([jnp.ones((1, piece_len), jnp.float32), passed_all[:-1]], 0), axis=0
    )
    my_color = jnp.sum(ordered[:, 0:3, :] * ahead_light[:, None, :], axis=0)
    through = jnp.prod(passed_all, axis=0)
    my_piece = jnp.concatenate([my_color, (1.0 - through)[None]], 0)
    full_tile = lax.all_gather(my_piece, "depth", axis=1, tiled=True)
    return full_tile.reshape(4, cols_x, cols_y)


def solution(mesh):
    return jax.shard_map(
        on_device,
        mesh=mesh,
        in_specs=(P("depth", "imgx", "imgy"), P("depth", "imgx", "imgy"), P(), P()),
        out_specs=P(None, "imgx", "imgy"),
        check_vma=False,
    )
```

profile of v0, /device:TPU:0, one launch (start us, length us, event | category | flops | bytes accessed | tf_op | source)
XLA Modules:
  0.0 172.7 jit_solution(10692280450666354)
XLA Ops:
  0.0 23.3 %while.11 = (s32[]{:T(128)}, f32[8,4,16384]{2,1,0:T(4,128)S(1)}, s32[8,128,128]{2,1,0:T(8,128)}, bf16[4,128]{1,0:T(4,128)(2,1)}, s32[]{:T(128)}) while((s32[]{:T(128)}, f32[8,4,16384]{2,1,0:T(4,128)S(1)}, s32[8,128,128]{2,1,0:T(8,128)}, bf16[4,128]{1,0:T(4,128)(2,1)}, s32[]{:T(128)}) %tuple.22), condition=%wide.region_1.2_spmd.clone, body=%wide.region_0.1_spmd.clone.sunk | while | flops 18874368 | bytes 459845 | solution.py:18
  0.0 0.9 dynamic-slice_bitcast_fusion.2
  0.9 2.1 %fusion.16 = f32[8,4,16384]{2,1,0:T(4,128)S(1)} fusion(f32[8,4,16384]{2,1,0:T(4,128)S(1)} %get-tuple-element.84, s32[]{:T(128)} %get-tuple-element.83, bf16[4,128]{1,0:T(4,128)(2,1)} %get-tuple-element.91, s32[16384]{0:T(1024)S(1)} %dynamic-slice_bitcast_fusion.2), kind=kOutput, calls=%fused_computation.3.clone.1 | convolution fusion | flops 18874368 | bytes 328708 | tf_op jit(solution)/shard_map/while/body/eval_jaxpr/dot_general | solution.py:16
  3.0 0.8 dynamic-slice_bitcast_fusion.2
  3.8 2.1 %fusion.16 = f32[8,4,16384]{2,1,0:T(4,128)S(1)} fusion(f32[8,4,16384]{2,1,0:T(4,128)S(1)} %get-tuple-element.84, s32[]{:T(128)} %get-tuple-element.83, bf16[4,128]{1,0:T(4,128)(2,1)} %get-tuple-element.91, s32[16384]{0:T(1024)S(1)} %dynamic-slice_bitcast_fusion.2), kind=kOutput, calls=%fused_computation.3.clone.1 | convolution fusion | flops 18874368 | bytes 328708 | tf_op jit(solution)/shard_map/while/body/eval_jaxpr/dot_general | solution.py:16
  6.7 2.1 %fusion.16 = f32[8,4,16384]{2,1,0:T(4,128)S(1)} fusion(f32[8,4,16384]{2,1,0:T(4,128)S(1)} %get-tuple-element.84, s32[]{:T(128)} %get-tuple-element.83, bf16[4,128]{1,0:T(4,128)(2,1)} %get-tuple-element.91, s32[16384]{0:T(1024)S(1)} %dynamic-slice_bitcast_fusion.2), kind=kOutput, calls=%fused_computation.3.clone.1 | convolution fusion | flops 18874368 | bytes 328708 | tf_op jit(solution)/shard_map/while/body/eval_jaxpr/dot_general | solution.py:16
  9.6 2.1 %fusion.16 = f32[8,4,16384]{2,1,0:T(4,128)S(1)} fusion(f32[8,4,16384]{2,1,0:T(4,128)S(1)} %get-tuple-element.84, s32[]{:T(128)} %get-tuple-element.83, bf16[4,128]{1,0:T(4,128)(2,1)} %get-tuple-element.91, s32[16384]{0:T(1024)S(1)} %dynamic-slice_bitcast_fusion.2), kind=kOutput, calls=%fused_computation.3.clone.1 | convolution fusion | flops 18874368 | bytes 328708 | tf_op jit(solution)/shard_map/while/body/eval_jaxpr/dot_general | solution.py:16
  12.5 2.1 %fusion.16 = f32[8,4,16384]{2,1,0:T(4,128)S(1)} fusion(f32[8,4,16384]{2,1,0:T(4,128)S(1)} %get-tuple-element.84, s32[]{:T(128)} %get-tuple-element.83, bf16[4,128]{1,0:T(4,128)(2,1)} %get-tuple-element.91, s32[16384]{0:T(1024)S(1)} %dynamic-slice_bitcast_fusion.2), kind=kOutput, calls=%fused_computation.3.clone.1 | convolution fusion | flops 18874368 | bytes 328708 | tf_op jit(solution)/shard_map/while/body/eval_jaxpr/dot_general | solution.py:16
  14.6 0.8 dynamic-slice_bitcast_fusion.2
  15.4 2.1 %fusion.16 = f32[8,4,16384]{2,1,0:T(4,128)S(1)} fusion(f32[8,4,16384]{2,1,0:T(4,128)S(1)} %get-tuple-element.84, s32[]{:T(128)} %get-tuple-element.83, bf16[4,128]{1,0:T(4,128)(2,1)} %get-tuple-element.91, s32[16384]{0:T(1024)S(1)} %dynamic-slice_bitcast_fusion.2), kind=kOutput, calls=%fused_computation.3.clone.1 | convolution fusion | flops 18874368 | bytes 328708 | tf_op jit(solution)/shard_map/while/body/eval_jaxpr/dot_general | solution.py:16
  18.3 2.1 %fusion.16 = f32[8,4,16384]{2,1,0:T(4,128)S(1)} fusion(f32[8,4,16384]{2,1,0:T(4,128)S(1)} %get-tuple-element.84, s32[]{:T(128)} %get-tuple-element.83, bf16[4,128]{1,0:T(4,128)(2,1)} %get-tuple-element.91, s32[16384]{0:T(1024)S(1)} %dynamic-slice_bitcast_fusion.2), kind=kOutput, calls=%fused_computation.3.clone.1 | convolution fusion | flops 18874368 | bytes 328708 | tf_op jit(solution)/shard_map/while/body/eval_jaxpr/dot_general | solution.py:16
  20.4 0.8 dynamic-slice_bitcast_fusion.2
  21.2 2.1 %fusion.16 = f32[8,4,16384]{2,1,0:T(4,128)S(1)} fusion(f32[8,4,16384]{2,1,0:T(4,128)S(1)} %get-tuple-element.84, s32[]{:T(128)} %get-tuple-element.83, bf16[4,128]{1,0:T(4,128)(2,1)} %get-tuple-element.91, s32[16384]{0:T(1024)S(1)} %dynamic-slice_bitcast_fusion.2), kind=kOutput, calls=%fused_computation.3.clone.1 | convolution fusion | flops 18874368 | bytes 328708 | tf_op jit(solution)/shard_map/while/body/eval_jaxpr/dot_general | solution.py:16
  23.9 1.2 fusion.6
  26.6 0.9 multiply_reduce_fusion
  27.6 5.1 %copy.8 = f32[4,16384]{0,1:T(8,128)} copy(f32[4,16384]{1,0:T(4,128)S(1)} %pad_maximum_fusion) | data formatting | bytes 524288 | tf_op jit(solution)/shard_map/concatenate | solution.py:27
  33.2 74.4 %reduce.1 = f32[16384,4]{1,0:T(8,128)} reduce(f32[16384,1,4]{2,1,0:T(1,128)} %bitcast.46, f32[]{:T(128)} %broadcast.39), dimensions={1}, to_apply=%bitcast.33.reduce_sub_computation | reduce | bytes 524292
  107.6 9.1 %reshape.72 = f32[4,1,16384]{2,1,0:T(1,128)} reshape(f32[16384,4]{1,0:T(8,128)} %reduce.1) | data formatting | bytes 524288
  116.7 6.3 %all-to-all-start = ((f32[4,1,16384]{2,1,0:T(1,128)}), f32[4,1,16384]{2,1,0:T(1,128)S(1)}, u32[]{:S(2)}, u32[]{:S(2)}) async-start(f32[4,1,16384]{2,1,0:T(1,128)} %reshape.72), calls=%async_computation | async-start | bytes 524288 | tf_op jit(solution)/shard_map/all_to_all | solution.py:28
  123.0 8.9 %all-to-all-done = f32[4,1,16384]{2,1,0:T(1,128)S(1)} async-done(((f32[4,1,16384]{2,1,0:T(1,128)}), f32[4,1,16384]{2,1,0:T(1,128)S(1)}, u32[]{:S(2)}, u32[]{:S(2)}) %all-to-all-start) | async-done | bytes 262176 | tf_op jit(solution)/shard_map/all_to_all | solution.py:28
  131.9 1.3 reduce.2
  133.2 17.7 %reshape.73 = f32[16384,1,4]{2,1,0:T(1,128)} reshape(f32[4,16384]{1,0:T(4,128)S(1)} %reduce.2) | data formatting | bytes 524288
  150.9 5.3 %copy.10 = f32[1,4,4,4096]{3,1,2,0:T(4,128)S(1)} copy(f32[1,4,4,4096]{1,3,2,0:T(8,128)} %bitcast.47) | data formatting | bytes 524288 | tf_op jit(solution)/shard_map/all_to_all | solution.py:28
  157.5 14.5 %all_gather.3 = f32[4,16384]{1,0:T(4,128)S(1)} all-gather(f32[4,4096]{1,0:T(4,128)S(1)} %pad_maximum_fusion.1), channel_id=1, replica_groups=mesh['depth'=4,'imgx'=4,'imgy'=2] {'depth'}, dimensions={1}, use_global_device_ids=true | all-gather | bytes 327680 | tf_op jit(solution)/shard_map/all_gather | solution.py:37
  (30 shorter events, 8.0 us)
Async XLA Ops:
  0.0 23.3 %copy-start = (bf16[8,128,128]{2,1,0:T(8,128)(2,1)S(1)}, bf16[8,128,128]{2,1,0:T(8,128)(2,1)}, u32[]{:S(2)}) copy-start(bf16[8,128,128]{2,1,0:T(8,128)(2,1)} %param.6) | copy-start | bytes 786436
  107.6 15.4 %copy-start.1 = (s32[4]{0:T(128)S(1)}, s32[4]{0:T(128)}, u32[]{:S(2)}) copy-start(s32[4]{0:T(128)} %param.9) | copy-start | bytes 52
  116.7 15.3 %all-to-all-start = ((f32[4,1,16384]{2,1,0:T(1,128)}), f32[4,1,16384]{2,1,0:T(1,128)S(1)}, u32[]{:S(2)}, u32[]{:S(2)}) async-start(f32[4,1,16384]{2,1,0:T(1,128)} %reshape.72), calls=%async_computation | async-start | bytes 524288 | tf_op jit(solution)/shard_map/all_to_all | solution.py:28
where the time goes:
time: 173 us
  other arithmetic  79.2 us (46%)
  local copies, waits for them, and re-layouts  47.1 us (27%)
  matrix products  16.5 us (10%)
  blocking collectives  14.5 us (8%)
  waiting for transfers between devices  8.87 us (5%)
  starting transfers between devices  6.35 us (4%)
    unnamed x1, other arithmetic  74.4 us
    unnamed x11, local copies, waits for them, and re-layouts  28.7 us
    dot_general x8, matrix products, lookup(): return jnp.dot(color_table, onehot, preferred_element_type=jnp.float32)  16.5 us
    all_gather x1, blocking collectives, on_device(): full_tile = lax.all_gather(my_piece, 'depth', axis=1, tiled=True)  14.5 us
    all_to_all x1, waiting for transfers between devices, on_device(): lax.all_to_all(stacked, 'depth', split_axis=2, concat_axis=0, tiled=True)  8.87 us
    eq x8, local copies, waits for them, and re-layouts, lookup(): layer_bins.reshape(1, pixels) == levels[:, None]  6.79 us
    all_to_all x1, starting transfers between devices, on_device(): lax.all_to_all(stacked, 'depth', split_axis=2, concat_axis=0, tiled=True)  6.35 us
    all_to_all x1, local copies, waits for them, and re-layouts, on_device(): lax.all_to_all(stacked, 'depth', split_axis=2, concat_axis=0, tiled=True)  5.3 us
  transfers between devices with their start and end apart: 1, of which 1 were waited for; matrix products, arithmetic and copies ran while one was open for 0% of the time, Pallas kernels for 0%

commit v1 on v0

v1 whole, which is shorter than its diff:
```python
import functools
import math

import jax
import jax.numpy as jnp
from jax import lax
from jax.experimental import pallas as pl
from jax.experimental.pallas import tpu as pltpu
from jax.sharding import PartitionSpec as P

LANES = 128
LANE_GATHER = lax.GatherDimensionNumbers(
    offset_dims=(),
    collapsed_slice_dims=(1,),
    start_index_map=(1,),
    operand_batching_dims=(0,),
    start_indices_batching_dims=(0,),
)


def lane_lookup(table, index):
    return lax.gather(
        table,
        index[..., None],
        LANE_GATHER,
        slice_sizes=(1, 1),
        mode=lax.GatherScatterMode.PROMISE_IN_BOUNDS,
    )


def table_lookup(chunks, bins):
    if len(chunks) == 1:
        return lane_lookup(chunks[0], bins)
    low = bins % LANES
    high = bins // LANES
    out = lane_lookup(chunks[0], low)
    for c in range(1, len(chunks)):
        out = jnp.where(high == c, lane_lookup(chunks[c], low), out)
    return out


def load_table(table_ref, rows, rate_scale):
    channels, bins = table_ref.shape
    table = table_ref[...].astype(jnp.float32)
    chunks = []
    for ch in range(channels):
        row = table[ch : ch + 1, :]
        if ch == channels - 1:
            row = row * rate_scale
        chunks.append(
            [jnp.broadcast_to(row[:, c : c + LANES], (rows, LANES)) for c in range(0, bins, LANES)]
        )
    return chunks


def block_partial(emis_ref, bins_ref, chunks, row, rows, col, ray_step):
    depth_cells = emis_ref.shape[0]
    color = [None] * 3
    depth_sum = None
    for k in range(depth_cells):
        bright = emis_ref[k, pl.ds(row, rows), col : col + LANES].astype(jnp.float32)
        bins = bins_ref[k, pl.ds(row, rows), col : col + LANES]
        rate = bright * table_lookup(chunks[3], bins)
        if k:
            bright = bright * jnp.exp2(depth_sum)
        depth_sum = rate if depth_sum is None else depth_sum + rate
        for ch in range(3):
            term = bright * table_lookup(chunks[ch], bins)
            color[ch] = term if color[ch] is None else color[ch] + term
    return [c * ray_step for c in color] + [jnp.exp2(depth_sum)]


def partial_kernel(emis_ref, bins_ref, table_ref, *out_refs, ray_step, rows):
    me = lax.axis_index("depth")
    piece_rows, cols = out_refs[0].shape[1:]
    chunks = load_table(table_ref, rows, -ray_step * math.log2(math.e))
    for s, out_ref in enumerate(out_refs):
        first = (me ^ s) * piece_rows
        for r in range(0, piece_rows, rows):
            for col in range(0, cols, LANES):
                row = pl.multiple_of(first + r, rows)
                planes = block_partial(emis_ref, bins_ref, chunks, row, rows, col, ray_step)
                for ch, plane in enumerate(planes):
                    out_ref[ch, r : r + rows, col : col + LANES] = plane


def composite_kernel(order_ref, *refs):
    me = lax.axis_index("depth")
    in_refs, out_ref = refs[:-1], refs[-1]
    n = len(in_refs)

    def pick(slot, ch):
        value = in_refs[0][ch]
        for s in range(1, n):
            value = jnp.where(slot == s, in_refs[s][ch], value)
        return value

    color = [None] * 3
    through = None
    for k in range(n):
        slot = me ^ order_ref[k]
        for ch in range(3):
            term = pick(slot, ch)
            if k:
                term = color[ch] + through * term
            color[ch] = term
        passed = pick(slot, 3)
        through = passed if through is None else through * passed
    for ch in range(3):
        out_ref[ch] = color[ch]
    out_ref[3] = 1.0 - through


def assemble_kernel(*refs):
    me = lax.axis_index("depth")
    in_refs, out_ref = refs[:-1], refs[-1]
    piece_rows = in_refs[0].shape[1]
    for s, in_ref in enumerate(in_refs):
        row = pl.multiple_of((me ^ s) * piece_rows, piece_rows)
        out_ref[:, pl.ds(row, piece_rows), :] = in_ref[...]


def exchange(pieces, devices):
    received = [None] * devices
    for s in reversed(range(1, devices)):
        received[s] = lax.ppermute(pieces[s], "depth", [(d, d ^ s) for d in range(devices)])
    return received


VMEM = pl.BlockSpec(memory_space=pltpu.VMEM)
SMEM = pl.BlockSpec(memory_space=pltpu.SMEM)


def by_exchange(emissivity, bin_index, color_table, brick_order, devices, ray_step):
    depth_cells, cols_x, cols_y = emissivity.shape
    piece_rows = cols_x // devices
    rows = 16 if piece_rows % 16 == 0 else 8
    piece = jax.ShapeDtypeStruct((4, piece_rows, cols_y), jnp.float32)
    pieces = pl.pallas_call(
        functools.partial(partial_kernel, ray_step=ray_step, rows=rows),
        out_shape=[piece] * devices,
        in_specs=[VMEM, VMEM, VMEM],
        out_specs=[VMEM] * devices,
        name="partial",
    )(emissivity, bin_index, color_table)
    received = exchange(pieces, devices)
    received[0] = pieces[0]
    mine = pl.pallas_call(
        composite_kernel,
        out_shape=piece,
        in_specs=[SMEM] + [VMEM] * devices,
        out_specs=VMEM,
        name="composite",
    )(brick_order, *received)
    tiles = exchange([mine] * devices, devices)
    tiles[0] = mine
    return pl.pallas_call(
        assemble_kernel,
        out_shape=jax.ShapeDtypeStruct((4, cols_x, cols_y), jnp.float32),
        in_specs=[VMEM] * devices,
        out_specs=VMEM,
        name="assemble",
    )(*tiles)


def whole_partial_kernel(emis_ref, bins_ref, table_ref, out_ref, *, ray_step, rows):
    chunks = load_table(table_ref, rows, -ray_step * math.log2(math.e))
    cols_x, cols_y = out_ref.shape[1:]

    def step(b, carry):
        row = pl.multiple_of(b * rows, rows)
        for col in range(0, cols_y, LANES):
            planes = block_partial(emis_ref, bins_ref, chunks, row, rows, col, ray_step)
            for ch, plane in enumerate(planes):
                out_ref[ch, pl.ds(row, rows), col : col + LANES] = plane
        return carry

    lax.fori_loop(0, cols_x // rows, step, 0)


def by_collectives(emissivity, bin_index, color_table, brick_order, devices, ray_step):
    depth_cells, cols_x, cols_y = emissivity.shape
    partials = pl.pallas_call(
        functools.partial(whole_partial_kernel, ray_step=ray_step, rows=8),
        out_shape=jax.ShapeDtypeStruct((4, cols_x, cols_y), jnp.float32),
        in_specs=[VMEM, VMEM, VMEM],
        out_specs=VMEM,
        name="partial_whole",
    )(emissivity, bin_index, color_table)
    pieces = partials.reshape(4, devices, cols_x // devices, cols_y).transpose(1, 0, 2, 3)
    received = lax.all_to_all(pieces, "depth", split_axis=0, concat_axis=0, tiled=True)

    def advance(state, brick):
        color, through = state
        planes = lax.dynamic_index_in_dim(received, brick, 0, keepdims=False)
        return (color + through * planes[0:3], through * planes[3]), None

    start = (jnp.zeros_like(received[0, 0:3]), jnp.ones_like(received[0, 3]))
    (color, through), _ = lax.scan(advance, start, brick_order)
    mine = jnp.concatenate([color, (1.0 - through)[None]], 0)
    return lax.all_gather(mine, "depth", axis=1, tiled=True)


def on_device(emissivity, bin_index, color_table, brick_order):
    depth_cells, cols_x, cols_y = emissivity.shape
    devices = lax.axis_size("depth")
    ray_step = 2.0 / (depth_cells * devices)
    few = devices <= 8 and devices & (devices - 1) == 0 and cols_x % (8 * devices) == 0
    plan = by_exchange if few else by_collectives
    return plan(emissivity, bin_index, color_table, brick_order, devices, ray_step)


def solution(mesh):
    return jax.shard_map(
        on_device,
        mesh=mesh,
        in_specs=(P("depth", "imgx", "imgy"), P("depth", "imgx", "imgy"), P(), P()),
        out_specs=P(None, "imgx", "imgy"),
        check_vma=False,
    )
```

time: 173 us -> 28 us (0.16)
  other arithmetic: 79.2 us -> 0 us
  local copies, waits for them, and re-layouts: 47.1 us -> 1.85 us
  matrix products: 16.5 us -> 0 us
  blocking collectives: 14.5 us -> 0 us
  Pallas kernels: 0 us -> 6.27 us
  starting transfers between devices: 6.35 us -> 10 us
    unnamed x1 -> x0, other arithmetic: 74.4 us -> none
    unnamed x11 -> x12, local copies, waits for them, and re-layouts: 28.7 us -> 1.85 us
    dot_general x8 -> x0, matrix products: 16.5 us -> none  [lookup(): return jnp.dot(color_table, onehot, preferred_element_type=jnp.float32)]
    all_gather x1 -> x0, blocking collectives: 14.5 us -> none  [on_device(): full_tile = lax.all_gather(my_piece, 'depth', axis=1, tiled=True)]
    ppermute x0 -> x6, starting transfers between devices: none -> 10 us  [exchange(): lax.ppermute(pieces[s], 'depth', [(d, d ^ s) for d in range(devices)])]
    ppermute x0 -> x6, waiting for transfers between devices: none -> 9.56 us  [exchange(): lax.ppermute(pieces[s], 'depth', [(d, d ^ s) for d in range(devices)])]
    all_to_all x1 -> x0, waiting for transfers between devices: 8.87 us -> none  [on_device(): lax.all_to_all(stacked, 'depth', split_axis=2, concat_axis=0, tiled=True)]
    eq x8 -> x0, local copies, waits for them, and re-layouts: 6.79 us -> none  [lookup(): layer_bins.reshape(1, pixels) == levels[:, None]]
  transfers between devices with their start and end apart: 1 -> 6, of which waited for: 1 -> 4; matrix products, arithmetic and copies ran while one was open for 0% -> 0% of each run, Pallas kernels for 0% -> 0%
where the time goes in v1:
time: 28 us; the launch traced here: 27.7 us
  starting transfers between devices  10 us (36%)
  waiting for transfers between devices  9.56 us (34%)
  Pallas kernels  6.27 us (22%)
  local copies, waits for them, and re-layouts  1.85 us (7%)
    ppermute x6, starting transfers between devices, exchange(): lax.ppermute(pieces[s], 'depth', [(d, d ^ s) for d in range(devices)])  10 us
    ppermute x6, waiting for transfers between devices, exchange(): lax.ppermute(pieces[s], 'depth', [(d, d ^ s) for d in range(devices)])  9.56 us
    pallas_call x1, Pallas kernels, by_exchange(): pl.pallas_call(functools.partial(partial_kernel, ray_step=ray_step, rows=...  2.98 us
    unnamed x12, local copies, waits for them, and re-layouts  1.85 us
    pallas_call x1, Pallas kernels, by_exchange(): pl.pallas_call(assemble_kernel, out_shape=jax.ShapeDtypeStruct((4, cols_x...  1.66 us
    pallas_call x1, Pallas kernels, by_exchange(): pl.pallas_call(composite_kernel, out_shape=piece, in_specs=[SMEM] + [VMEM...  1.63 us
  transfers between devices with their start and end apart: 6, of which 4 were waited for; matrix products, arithmetic and copies ran while one was open for 0% of the time, Pallas kernels for 0%

profile of v1, /device:TPU:0, one launch (start us, length us, event | category | flops | bytes accessed | tf_op | source)
XLA Modules:
  0.0 27.7 jit_solution(14973013499582430198)
XLA Ops:
  0.0 3.0 %partial.1 = (f32[4,32,128]{2,1,0:T(8,128)}, f32[4,32,128]{2,1,0:T(8,128)}, f32[4,32,128]{2,1,0:T(8,128)}, f32[4,32,128]{2,1,0:T(8,128)}) custom-call(bf16[8,128,128]{2,1,0:T(8,128)(2,1)} %emis_ref.1, s32[8,128,128]{2,1,0:T(8,128)} %bins_ref.1, bf16[4,128]{1,0:T(4,128)(2,1)} %table_ref.1), custom_call_target="tpu_custom_call" | custom-call | tf_op jit(solution)/shard_map/partial/pallas_call | solution.py:139
  3.0 3.1 %collective-permute-start = (f32[4,32,128]{2,1,0:T(8,128)}, f32[4,32,128]{2,1,0:T(8,128)S(1)}, u32[]{:S(2)}, u32[]{:S(2)}) collective-permute-start(f32[4,32,128]{2,1,0:T(8,128)} %get-tuple-element.10), channel_id=1, source_target_pairs={{0,8},{8,0},{16,24},{24,16},{1,9},{9,1},{17,25},{25,17},{2,10},{10... | collective-permute-start | bytes 196616 | tf_op jit(solution)/shard_map/ppermute | solution.py:126
  6.0 2.6 %collective-permute-start.1 = (f32[4,32,128]{2,1,0:T(8,128)}, f32[4,32,128]{2,1,0:T(8,128)S(1)}, u32[]{:S(2)}, u32[]{:S(2)}) collective-permute-start(f32[4,32,128]{2,1,0:T(8,128)} %get-tuple-element.11), channel_id=1, source_target_pairs={{0,16},{8,24},{16,0},{24,8},{1,17},{9,25},{17,1},{25,9},{2,18},{10... | collective-permute-start | bytes 196616 | tf_op jit(solution)/shard_map/ppermute | solution.py:126
  8.6 0.0 collective-permute-start.2
  8.6 0.0 collective-permute-done.refs_1_
  8.6 0.0 copy-start
  8.6 4.9 %collective-permute-done.1.refs_2_ = f32[4,32,128]{2,1,0:T(8,128)S(1)} collective-permute-done((f32[4,32,128]{2,1,0:T(8,128)}, f32[4,32,128]{2,1,0:T(8,128)S(1)}, u32[]{:S(2)}, u32[]{:S(2)}) %collective-permute-start.1) | collective-permute-done | bytes 65568 | tf_op jit(solution)/shard_map/ppermute | solution.py:126
  13.5 0.0 copy-start.1
  13.5 1.4 %collective-permute-done.2.refs_3_ = f32[4,32,128]{2,1,0:T(8,128)S(1)} collective-permute-done((f32[4,32,128]{2,1,0:T(8,128)}, f32[4,32,128]{2,1,0:T(8,128)S(1)}, u32[]{:S(2)}, u32[]{:S(2)}) %collective-permute-start.2) | collective-permute-done | bytes 65568 | tf_op jit(solution)/shard_map/ppermute | solution.py:126
  14.9 0.0 copy-start.2
  14.9 0.0 copy-done
  14.9 0.0 copy-done.1
  14.9 0.6 %copy-done.2 = f32[4,32,128]{2,1,0:T(8,128)} copy-done((f32[4,32,128]{2,1,0:T(8,128)}, f32[4,32,128]{2,1,0:T(8,128)S(1)}, u32[]{:S(2)}) %copy-start.2) | copy-done | bytes 65560
  15.5 1.6 %composite.1.refs_0_ = f32[4,32,128]{2,1,0:T(8,128)} custom-call(s32[4]{0:T(128)} %order_ref.1, f32[4,32,128]{2,1,0:T(8,128)} %get-tuple-element.9.refs_0_, f32[4,32,128]{2,1,0:T(8,128)} %copy-done, f32[4,32,128]{2,1,0:T(8,128)} %copy-done.1, f32[4,32,128]{2,1,0:T(8,128)} %copy-done.2), custom_call_target="tpu_custom_call" | custom-call | tf_op jit(solution)/shard_map/composite/pallas_call | solution.py:148
  17.2 1.8 %collective-permute-start.5 = (f32[4,32,128]{2,1,0:T(8,128)}, f32[4,32,128]{2,1,0:T(8,128)S(1)}, u32[]{:S(2)}, u32[]{:S(2)}) collective-permute-start(f32[4,32,128]{2,1,0:T(8,128)} %composite.1.refs_0_), channel_id=1, source_target_pairs={{0,24},{8,16},{16,8},{24,0},{1,25},{9,17},{17,9},{25,1},{2,26},{10... | collective-permute-start | bytes 196616 | tf_op jit(solution)/shard_map/ppermute | solution.py:126
  19.0 0.0 collective-permute-start.4
  19.0 2.6 %collective-permute-start.3 = (f32[4,32,128]{2,1,0:T(8,128)}, f32[4,32,128]{2,1,0:T(8,128)S(1)}, u32[]{:S(2)}, u32[]{:S(2)}) collective-permute-start(f32[4,32,128]{2,1,0:T(8,128)} %composite.1.refs_0_), channel_id=1, source_target_pairs={{0,8},{8,0},{16,24},{24,16},{1,9},{9,1},{17,25},{25,17},{2,10},{10... | collective-permute-start | bytes 196616 | tf_op jit(solution)/shard_map/ppermute | solution.py:126
  21.5 1.9 %collective-permute-done.5.refs_3_ = f32[4,32,128]{2,1,0:T(8,128)S(1)} collective-permute-done((f32[4,32,128]{2,1,0:T(8,128)}, f32[4,32,128]{2,1,0:T(8,128)S(1)}, u32[]{:S(2)}, u32[]{:S(2)}) %collective-permute-start.5) | collective-permute-done | bytes 65568 | tf_op jit(solution)/shard_map/ppermute | solution.py:126
  23.4 1.4 %collective-permute-done.4.refs_2_ = f32[4,32,128]{2,1,0:T(8,128)S(1)} collective-permute-done((f32[4,32,128]{2,1,0:T(8,128)}, f32[4,32,128]{2,1,0:T(8,128)S(1)}, u32[]{:S(2)}, u32[]{:S(2)}) %collective-permute-start.4) | collective-permute-done | bytes 65568 | tf_op jit(solution)/shard_map/ppermute | solution.py:126
  24.8 0.0 collective-permute-done.3.refs_1_
  24.8 0.0 copy-done.3
  24.9 0.6 %copy-done.4 = f32[4,32,128]{2,1,0:T(8,128)} copy-done((f32[4,32,128]{2,1,0:T(8,128)}, f32[4,32,128]{2,1,0:T(8,128)S(1)}, u32[]{:S(2)}) %copy-start.4) | copy-done | bytes 65560
  25.5 0.6 %copy-done.5 = f32[4,32,128]{2,1,0:T(8,128)} copy-done((f32[4,32,128]{2,1,0:T(8,128)}, f32[4,32,128]{2,1,0:T(8,128)S(1)}, u32[]{:S(2)}) %copy-start.5) | copy-done | bytes 65560
  26.1 1.7 %assemble.1 = f32[4,128,128]{2,1,0:T(8,128)} custom-call(f32[4,32,128]{2,1,0:T(8,128)} %composite.1.refs_0_, f32[4,32,128]{2,1,0:T(8,128)} %copy-done.5, f32[4,32,128]{2,1,0:T(8,128)} %copy-done.4, f32[4,32,128]{2,1,0:T(8,128)} %copy-done.3), custom_call_target="tpu_custom_call" | custom-call | tf_op jit(solution)/shard_map/assemble/pallas_call | solution.py:157
  (3 shorter events, 0.0 us)
Async XLA Ops:
  3.0 5.6 %collective-permute-start = (f32[4,32,128]{2,1,0:T(8,128)}, f32[4,32,128]{2,1,0:T(8,128)S(1)}, u32[]{:S(2)}, u32[]{:S(2)}) collective-permute-start(f32[4,32,128]{2,1,0:T(8,128)} %get-tuple-element.10), channel_id=1, source_target_pairs={{0,8},{8,0},{16,24},{24,16},{1,9},{9,1},{17,25},{25,17},{2,10},{10... | collective-permute-start | bytes 196616 | tf_op jit(solution)/shard_map/ppermute | solution.py:126
  6.0 7.5 %collective-permute-start.1 = (f32[4,32,128]{2,1,0:T(8,128)}, f32[4,32,128]{2,1,0:T(8,128)S(1)}, u32[]{:S(2)}, u32[]{:S(2)}) collective-permute-start(f32[4,32,128]{2,1,0:T(8,128)} %get-tuple-element.11), channel_id=1, source_target_pairs={{0,16},{8,24},{16,0},{24,8},{1,17},{9,25},{17,1},{25,9},{2,18},{10... | collective-permute-start | bytes 196616 | tf_op jit(solution)/shard_map/ppermute | solution.py:126
  8.6 6.3 %collective-permute-start.2 = (f32[4,32,128]{2,1,0:T(8,128)}, f32[4,32,128]{2,1,0:T(8,128)S(1)}, u32[]{:S(2)}, u32[]{:S(2)}) collective-permute-start(f32[4,32,128]{2,1,0:T(8,128)} %get-tuple-element.12), channel_id=1, source_target_pairs={{0,24},{8,16},{16,8},{24,0},{1,25},{9,17},{17,9},{25,1},{2,26},{10... | collective-permute-start | bytes 196616 | tf_op jit(solution)/shard_map/ppermute | solution.py:126
  8.6 6.3 %copy-start = (f32[4,32,128]{2,1,0:T(8,128)}, f32[4,32,128]{2,1,0:T(8,128)S(1)}, u32[]{:S(2)}) copy-start(f32[4,32,128]{2,1,0:T(8,128)S(1)} %collective-permute-done.refs_1_) | copy-start | bytes 196612
  13.5 1.4 %copy-start.1 = (f32[4,32,128]{2,1,0:T(8,128)}, f32[4,32,128]{2,1,0:T(8,128)S(1)}, u32[]{:S(2)}) copy-start(f32[4,32,128]{2,1,0:T(8,128)S(1)} %collective-permute-done.1.refs_2_) | copy-start | bytes 196612
  14.9 0.6 %copy-start.2 = (f32[4,32,128]{2,1,0:T(8,128)}, f32[4,32,128]{2,1,0:T(8,128)S(1)}, u32[]{:S(2)}) copy-start(f32[4,32,128]{2,1,0:T(8,128)S(1)} %collective-permute-done.2.refs_3_) | copy-start | bytes 196612
  17.2 6.3 %collective-permute-start.5 = (f32[4,32,128]{2,1,0:T(8,128)}, f32[4,32,128]{2,1,0:T(8,128)S(1)}, u32[]{:S(2)}, u32[]{:S(2)}) collective-permute-start(f32[4,32,128]{2,1,0:T(8,128)} %composite.1.refs_0_), channel_id=1, source_target_pairs={{0,24},{8,16},{16,8},{24,0},{1,25},{9,17},{17,9},{25,1},{2,26},{10... | collective-permute-start | bytes 196616 | tf_op jit(solution)/shard_map/ppermute | solution.py:126
  19.0 5.9 %collective-permute-start.4 = (f32[4,32,128]{2,1,0:T(8,128)}, f32[4,32,128]{2,1,0:T(8,128)S(1)}, u32[]{:S(2)}, u32[]{:S(2)}) collective-permute-start(f32[4,32,128]{2,1,0:T(8,128)} %composite.1.refs_0_), channel_id=1, source_target_pairs={{0,16},{8,24},{16,0},{24,8},{1,17},{9,25},{17,1},{25,9},{2,18},{10... | collective-permute-start | bytes 196616 | tf_op jit(solution)/shard_map/ppermute | solution.py:126
  19.0 5.9 %collective-permute-start.3 = (f32[4,32,128]{2,1,0:T(8,128)}, f32[4,32,128]{2,1,0:T(8,128)S(1)}, u32[]{:S(2)}, u32[]{:S(2)}) collective-permute-start(f32[4,32,128]{2,1,0:T(8,128)} %composite.1.refs_0_), channel_id=1, source_target_pairs={{0,8},{8,0},{16,24},{24,16},{1,9},{9,1},{17,25},{25,17},{2,10},{10... | collective-permute-start | bytes 196616 | tf_op jit(solution)/shard_map/ppermute | solution.py:126
  23.4 1.4 %copy-start.3 = (f32[4,32,128]{2,1,0:T(8,128)}, f32[4,32,128]{2,1,0:T(8,128)S(1)}, u32[]{:S(2)}) copy-start(f32[4,32,128]{2,1,0:T(8,128)S(1)} %collective-permute-done.5.refs_3_) | copy-start | bytes 196612
  24.8 0.6 %copy-start.4 = (f32[4,32,128]{2,1,0:T(8,128)}, f32[4,32,128]{2,1,0:T(8,128)S(1)}, u32[]{:S(2)}) copy-start(f32[4,32,128]{2,1,0:T(8,128)S(1)} %collective-permute-done.4.refs_2_) | copy-start | bytes 196612
  25.5 0.6 %copy-start.5 = (f32[4,32,128]{2,1,0:T(8,128)}, f32[4,32,128]{2,1,0:T(8,128)S(1)}, u32[]{:S(2)}) copy-start(f32[4,32,128]{2,1,0:T(8,128)S(1)} %collective-permute-done.3.refs_1_) | copy-start | bytes 196612

commit v2 on v1

--- a/solution.py
+++ b/solution.py
@@ -113,11 +113,18 @@
 
 def assemble_kernel(*refs):
     me = lax.axis_index("depth")
-    in_refs, out_ref = refs[:-1], refs[-1]
+    in_refs, out_ref, sems = refs[:-2], refs[-2], refs[-1]
     piece_rows = in_refs[0].shape[1]
+    copies = []
     for s, in_ref in enumerate(in_refs):
         row = pl.multiple_of((me ^ s) * piece_rows, piece_rows)
-        out_ref[:, pl.ds(row, piece_rows), :] = in_ref[...]
+        copies.append(
+            pltpu.make_async_copy(in_ref, out_ref.at[:, pl.ds(row, piece_rows), :], sems.at[s])
+        )
+    for copy in copies:
+        copy.start()
+    for copy in copies:
+        copy.wait()
 
 
 def exchange(pieces, devices):
@@ -129,13 +136,18 @@
 
 VMEM = pl.BlockSpec(memory_space=pltpu.VMEM)
 SMEM = pl.BlockSpec(memory_space=pltpu.SMEM)
+ANY = pl.BlockSpec(memory_space=pl.ANY)
+
+
+def in_vmem(arrays):
+    return [pltpu.with_memory_space_constraint(a, pltpu.VMEM) for a in arrays]
 
 
 def by_exchange(emissivity, bin_index, color_table, brick_order, devices, ray_step):
     depth_cells, cols_x, cols_y = emissivity.shape
     piece_rows = cols_x // devices
     rows = 16 if piece_rows % 16 == 0 else 8
-    piece = jax.ShapeDtypeStruct((4, piece_rows, cols_y), jnp.float32)
+    piece = pltpu.VMEM((4, piece_rows, cols_y), jnp.float32)
     pieces = pl.pallas_call(
         functools.partial(partial_kernel, ray_step=ray_step, rows=rows),
         out_shape=[piece] * devices,
@@ -151,16 +163,17 @@
         in_specs=[SMEM] + [VMEM] * devices,
         out_specs=VMEM,
         name="composite",
-    )(brick_order, *received)
+    )(brick_order, *in_vmem(received))
     tiles = exchange([mine] * devices, devices)
     tiles[0] = mine
     return pl.pallas_call(
         assemble_kernel,
         out_shape=jax.ShapeDtypeStruct((4, cols_x, cols_y), jnp.float32),
         in_specs=[VMEM] * devices,
-        out_specs=VMEM,
+        out_specs=ANY,
+        scratch_shapes=[pltpu.SemaphoreType.DMA((devices,))],
         name="assemble",
-    )(*tiles)
+    )(*in_vmem(tiles))
 
 
 def whole_partial_kernel(emis_ref, bins_ref, table_ref, out_ref, *, ray_step, rows):

time: 28 us -> 23.3 us (0.83)
  Pallas kernels: 6.27 us -> 3.79 us
  local copies, waits for them, and re-layouts: 1.85 us -> 0 us
  waiting for transfers between devices: 9.56 us -> 9.15 us
    unnamed x12 -> x0, local copies, waits for them, and re-layouts: 1.85 us -> none
    pallas_call x1, Pallas kernels: 1.66 us -> 0.73 us  [by_exchange(): pl.pallas_call(assemble_kernel, out_shape=jax.ShapeDtypeStruct((4, cols_x...]
    pallas_call x1, Pallas kernels: 1.63 us -> 0.72 us  [by_exchange(): pl.pallas_call(composite_kernel, out_shape=piece, in_specs=[SMEM] + [VMEM...]
    pallas_call x1, Pallas kernels: 2.98 us -> 2.34 us  [by_exchange(): pl.pallas_call(functools.partial(partial_kernel, ray_step=ray_step, rows=...]
    ppermute x6, waiting for transfers between devices: 9.56 us -> 9.15 us  [exchange(): lax.ppermute(pieces[s], 'depth', [(d, d ^ s) for d in range(devices)])]
where the time goes in v2:
time: 23.3 us; the launch traced here: 23.1 us
  starting transfers between devices  10.2 us (44%)
  waiting for transfers between devices  9.15 us (39%)
  Pallas kernels  3.79 us (16%)
    ppermute x6, starting transfers between devices, exchange(): lax.ppermute(pieces[s], 'depth', [(d, d ^ s) for d in range(devices)])  10.2 us
    ppermute x6, waiting for transfers between devices, exchange(): lax.ppermute(pieces[s], 'depth', [(d, d ^ s) for d in range(devices)])  9.15 us
    pallas_call x1, Pallas kernels, by_exchange(): pl.pallas_call(functools.partial(partial_kernel, ray_step=ray_step, rows=...  2.34 us
    pallas_call x1, Pallas kernels, by_exchange(): pl.pallas_call(assemble_kernel, out_shape=jax.ShapeDtypeStruct((4, cols_x...  0.73 us
    pallas_call x1, Pallas kernels, by_exchange(): pl.pallas_call(composite_kernel, out_shape=piece, in_specs=[SMEM] + [VMEM...  0.72 us
  transfers between devices with their start and end apart: 6, of which 4 were waited for; matrix products, arithmetic and copies ran while one was open for 0% of the time, Pallas kernels for 0%

profile of v2, /device:TPU:0, one launch (start us, length us, event | category | flops | bytes accessed | tf_op | source)
XLA Modules:
  0.0 23.1 jit_solution(532161043997145534)
XLA Ops:
  0.0 2.3 %partial.1 = (f32[4,32,128]{2,1,0:T(8,128)S(1)}, f32[4,32,128]{2,1,0:T(8,128)S(1)}, f32[4,32,128]{2,1,0:T(8,128)S(1)}, f32[4,32,128]{2,1,0:T(8,128)S(1)}) custom-call(bf16[8,128,128]{2,1,0:T(8,128)(2,1)} %emis_ref.1, s32[8,128,128]{2,1,0:T(8,128)} %bins_ref.1, bf16[4,128]{1,0:T(4,128)(2,1)} %table_ref.1), custom_call_target="tpu_custom_call" | custom-call | tf_op jit(solution)/shard_map/partial/pallas_call | solution.py:151
  2.3 3.1 %collective-permute-start = (f32[4,32,128]{2,1,0:T(8,128)S(1)}, f32[4,32,128]{2,1,0:T(8,128)S(1)}, u32[]{:S(2)}, u32[]{:S(2)}) collective-permute-start(f32[4,32,128]{2,1,0:T(8,128)S(1)} %get-tuple-element.10), channel_id=1, source_target_pairs={{0,8},{8,0},{16,24},{24,16},{1,9},{9,1},{17,25},{25,17},{2,10},{10... | collective-permute-start | bytes 196616 | tf_op jit(solution)/shard_map/ppermute | solution.py:133
  5.5 2.6 %collective-permute-start.1 = (f32[4,32,128]{2,1,0:T(8,128)S(1)}, f32[4,32,128]{2,1,0:T(8,128)S(1)}, u32[]{:S(2)}, u32[]{:S(2)}) collective-permute-start(f32[4,32,128]{2,1,0:T(8,128)S(1)} %get-tuple-element.11), channel_id=1, source_target_pairs={{0,16},{8,24},{16,0},{24,8},{1,17},{9,25},{17,1},{25,9},{2,18},{10... | collective-permute-start | bytes 196616 | tf_op jit(solution)/shard_map/ppermute | solution.py:133
  8.1 0.0 collective-permute-start.2
  8.1 0.0 collective-permute-done.refs_1_
  8.1 4.7 %collective-permute-done.1.refs_2_ = f32[4,32,128]{2,1,0:T(8,128)S(1)} collective-permute-done((f32[4,32,128]{2,1,0:T(8,128)S(1)}, f32[4,32,128]{2,1,0:T(8,128)S(1)}, u32[]{:S(2)}, u32[]{:S(2)}) %collective-permute-start.1) | collective-permute-done | bytes 65568 | tf_op jit(solution)/shard_map/ppermute | solution.py:133
  12.7 1.4 %collective-permute-done.2.refs_3_ = f32[4,32,128]{2,1,0:T(8,128)S(1)} collective-permute-done((f32[4,32,128]{2,1,0:T(8,128)S(1)}, f32[4,32,128]{2,1,0:T(8,128)S(1)}, u32[]{:S(2)}, u32[]{:S(2)}) %collective-permute-start.2) | collective-permute-done | bytes 65568 | tf_op jit(solution)/shard_map/ppermute | solution.py:133
  14.1 0.7 %composite.1.refs_0_ = f32[4,32,128]{2,1,0:T(8,128)S(1)} custom-call(s32[4]{0:T(128)} %order_ref.1, f32[4,32,128]{2,1,0:T(8,128)S(1)} %get-tuple-element.9.refs_0_, f32[4,32,128]{2,1,0:T(8,128)S(1)} %collective-permute-done.refs_1_, f32[4,32,128]{2,1,0:T(8,128)S(1)} %collective-permute-done.1.refs_2_, f32[4,32,128]{2,1,0:T(8,128)S(1)} %collective-permute-done.2.refs_3_), custom_call_target="tpu_custom_call" | custom-call | tf_op jit(solution)/shard_map/composite/pallas_call | solution.py:160
  14.9 1.8 %collective-permute-start.5 = (f32[4,32,128]{2,1,0:T(8,128)S(1)}, f32[4,32,128]{2,1,0:T(8,128)S(1)}, u32[]{:S(2)}, u32[]{:S(2)}) collective-permute-start(f32[4,32,128]{2,1,0:T(8,128)S(1)} %composite.1.refs_0_), channel_id=1, source_target_pairs={{0,24},{8,16},{16,8},{24,0},{1,25},{9,17},{17,9},{25,1},{2,26},{10... | collective-permute-start | bytes 196616 | tf_op jit(solution)/shard_map/ppermute | solution.py:133
  16.7 0.0 collective-permute-start.4
  16.7 2.6 %collective-permute-start.3 = (f32[4,32,128]{2,1,0:T(8,128)S(1)}, f32[4,32,128]{2,1,0:T(8,128)S(1)}, u32[]{:S(2)}, u32[]{:S(2)}) collective-permute-start(f32[4,32,128]{2,1,0:T(8,128)S(1)} %composite.1.refs_0_), channel_id=1, source_target_pairs={{0,8},{8,0},{16,24},{24,16},{1,9},{9,1},{17,25},{25,17},{2,10},{10... | collective-permute-start | bytes 196616 | tf_op jit(solution)/shard_map/ppermute | solution.py:133
  19.3 1.7 %collective-permute-done.5.refs_3_ = f32[4,32,128]{2,1,0:T(8,128)S(1)} collective-permute-done((f32[4,32,128]{2,1,0:T(8,128)S(1)}, f32[4,32,128]{2,1,0:T(8,128)S(1)}, u32[]{:S(2)}, u32[]{:S(2)}) %collective-permute-start.5) | collective-permute-done | bytes 65568 | tf_op jit(solution)/shard_map/ppermute | solution.py:133
  21.0 1.4 %collective-permute-done.4.refs_2_ = f32[4,32,128]{2,1,0:T(8,128)S(1)} collective-permute-done((f32[4,32,128]{2,1,0:T(8,128)S(1)}, f32[4,32,128]{2,1,0:T(8,128)S(1)}, u32[]{:S(2)}, u32[]{:S(2)}) %collective-permute-start.4) | collective-permute-done | bytes 65568 | tf_op jit(solution)/shard_map/ppermute | solution.py:133
  22.4 0.0 collective-permute-done.3.refs_1_
  22.4 0.7 %assemble.1 = f32[4,128,128]{2,1,0:T(8,128)} custom-call(f32[4,32,128]{2,1,0:T(8,128)S(1)} %composite.1.refs_0_, f32[4,32,128]{2,1,0:T(8,128)S(1)} %collective-permute-done.3.refs_1_, f32[4,32,128]{2,1,0:T(8,128)S(1)} %collective-permute-done.4.refs_2_, f32[4,32,128]{2,1,0:T(8,128)S(1)} %collective-permute-done.5.refs_3_), custom_call_target="tpu_custom_call" | custom-call | tf_op jit(solution)/shard_map/assemble/pallas_call | solution.py:169
Async XLA Ops:
  2.3 5.7 %collective-permute-start = (f32[4,32,128]{2,1,0:T(8,128)S(1)}, f32[4,32,128]{2,1,0:T(8,128)S(1)}, u32[]{:S(2)}, u32[]{:S(2)}) collective-permute-start(f32[4,32,128]{2,1,0:T(8,128)S(1)} %get-tuple-element.10), channel_id=1, source_target_pairs={{0,8},{8,0},{16,24},{24,16},{1,9},{9,1},{17,25},{25,17},{2,10},{10... | collective-permute-start | bytes 196616 | tf_op jit(solution)/shard_map/ppermute | solution.py:133
  5.5 7.3 %collective-permute-start.1 = (f32[4,32,128]{2,1,0:T(8,128)S(1)}, f32[4,32,128]{2,1,0:T(8,128)S(1)}, u32[]{:S(2)}, u32[]{:S(2)}) collective-permute-start(f32[4,32,128]{2,1,0:T(8,128)S(1)} %get-tuple-element.11), channel_id=1, source_target_pairs={{0,16},{8,24},{16,0},{24,8},{1,17},{9,25},{17,1},{25,9},{2,18},{10... | collective-permute-start | bytes 196616 | tf_op jit(solution)/shard_map/ppermute | solution.py:133
  8.1 6.1 %collective-permute-start.2 = (f32[4,32,128]{2,1,0:T(8,128)S(1)}, f32[4,32,128]{2,1,0:T(8,128)S(1)}, u32[]{:S(2)}, u32[]{:S(2)}) collective-permute-start(f32[4,32,128]{2,1,0:T(8,128)S(1)} %get-tuple-element.12), channel_id=1, source_target_pairs={{0,24},{8,16},{16,8},{24,0},{1,25},{9,17},{17,9},{25,1},{2,26},{10... | collective-permute-start | bytes 196616 | tf_op jit(solution)/shard_map/ppermute | solution.py:133
  14.9 6.1 %collective-permute-start.5 = (f32[4,32,128]{2,1,0:T(8,128)S(1)}, f32[4,32,128]{2,1,0:T(8,128)S(1)}, u32[]{:S(2)}, u32[]{:S(2)}) collective-permute-start(f32[4,32,128]{2,1,0:T(8,128)S(1)} %composite.1.refs_0_), channel_id=1, source_target_pairs={{0,24},{8,16},{16,8},{24,0},{1,25},{9,17},{17,9},{25,1},{2,26},{10... | collective-permute-start | bytes 196616 | tf_op jit(solution)/shard_map/ppermute | solution.py:133
  16.7 5.7 %collective-permute-start.4 = (f32[4,32,128]{2,1,0:T(8,128)S(1)}, f32[4,32,128]{2,1,0:T(8,128)S(1)}, u32[]{:S(2)}, u32[]{:S(2)}) collective-permute-start(f32[4,32,128]{2,1,0:T(8,128)S(1)} %composite.1.refs_0_), channel_id=1, source_target_pairs={{0,16},{8,24},{16,0},{24,8},{1,17},{9,25},{17,1},{25,9},{2,18},{10... | collective-permute-start | bytes 196616 | tf_op jit(solution)/shard_map/ppermute | solution.py:133
  16.7 5.7 %collective-permute-start.3 = (f32[4,32,128]{2,1,0:T(8,128)S(1)}, f32[4,32,128]{2,1,0:T(8,128)S(1)}, u32[]{:S(2)}, u32[]{:S(2)}) collective-permute-start(f32[4,32,128]{2,1,0:T(8,128)S(1)} %composite.1.refs_0_), channel_id=1, source_target_pairs={{0,8},{8,0},{16,24},{24,16},{1,9},{9,1},{17,25},{25,17},{2,10},{10... | collective-permute-start | bytes 196616 | tf_op jit(solution)/shard_map/ppermute | solution.py:133
